TPU v7x, 64 devices: a 2x2x8 block of a 4x4x8 slice. The times are simulated.
64 devices in a mesh: dp: 4 (over x, y), tp: 16 (over z, core).
Axes of the slice: x: 2, y: 2, z: 8, core: 2. Of those that a mesh axis runs over, the one named last changes fastest.
The devices are a block of a 4x4x8 slice.
Arguments:
- hidden: bfloat16 [1024, 8192], P('dp'), parts along dimension 0
- w_query: bfloat16 [8192, 8192], P(None, 'tp')
- w_key: bfloat16 [8192, 256], replicated
- w_value: bfloat16 [8192, 256], replicated
- w_out: bfloat16 [8192, 8192], P('tp')
- k_cache: bfloat16 [1024, 512, 256], P(('dp', 'tp')), parts along dimension 0
- v_cache: bfloat16 [1024, 512, 256], P(('dp', 'tp')), parts along dimension 0
- lengths: int32 [1024], P('dp'), parts along dimension 0
Outputs:
- output 1: bfloat16 [1024, 8192], P('dp', 'tp'), parts along dimension 0
- output 2: bfloat16 [1024, 512, 256], P(('dp', 'tp')), parts along dimension 0
- output 3: bfloat16 [1024, 512, 256], P(('dp', 'tp')), parts along dimension 0
There are 4 independent parts. A program takes and returns all parts, laid end to end along the dimension named above; an argument that names none is the same for every part.
All inputs are finite; a program needn't handle non-finite values.
Results may differ from a plain program's by a relative error of at most 0.0199816.
Values are sent between devices in bfloat16 or wider.
A program may use at most 768 MiB of HBM per device.

v0:
```python
import jax
import jax.numpy as jnp
from jax import lax
from jax.sharding import PartitionSpec as P


def rope_angles(positions, head_dim):
    half_dim = head_dim // 2
    inv_freq = 10000.0 ** (-(jnp.arange(half_dim, dtype=jnp.float32) * 2.0) / head_dim)
    return positions.astype(jnp.float32)[:, None] * inv_freq[None, :]


def apply_rope(values_in, angles):
    half_dim = values_in.shape[-1] // 2
    first_half = values_in[..., :half_dim]
    second_half = values_in[..., half_dim:]
    cosines = jnp.cos(angles)
    sines = jnp.sin(angles)
    return jnp.concatenate([first_half * cosines - second_half * sines, second_half * cosines + first_half * sines], axis=-1)


def attend(q_rot, k_all, v_all, lengths):
    head_dim = q_rot.shape[-1]
    seq_len = k_all.shape[1]
    scores = jnp.einsum('bhd,bsd->bhs', q_rot, k_all, preferred_element_type=jnp.float32) * (head_dim ** -0.5)
    valid_mask = lax.broadcasted_iota(jnp.int32, (1, 1, seq_len), 2) <= lengths[:, None, None]
    scores = jnp.where(valid_mask, scores, -1e30)
    row_max = jnp.max(scores, axis=-1, keepdims=True)
    weights = jnp.exp(scores - row_max)
    denominator = jnp.sum(weights, axis=-1, keepdims=True)
    summed = jnp.einsum('bhs,bsd->bhd', weights.astype(jnp.bfloat16), v_all, preferred_element_type=jnp.float32)
    return (summed / denominator).astype(jnp.bfloat16)


def solution(mesh):
    group_size = mesh.shape['tp']
    cache_spec = P(('dp', 'tp'), None, None)

    def local_step(hidden, w_query, w_key, w_value, w_out, k_cache, v_cache, lengths):
        rows_dev, seq_len, head_dim = k_cache.shape
        cols_dev = w_query.shape[1]
        num_heads = cols_dev * group_size // head_dim
        row_start = lax.axis_index('tp') * rows_dev
        q_cols = jnp.dot(hidden, w_query, preferred_element_type=jnp.float32).astype(jnp.bfloat16)
        q_rows = lax.all_to_all(q_cols, 'tp', 0, 1, tiled=True)
        own_hidden = lax.dynamic_slice_in_dim(hidden, row_start, rows_dev, axis=0)
        own_lengths = lax.dynamic_slice_in_dim(lengths, row_start, rows_dev, axis=0)
        k_new = jnp.dot(own_hidden, w_key, preferred_element_type=jnp.float32).astype(jnp.bfloat16)
        v_new = jnp.dot(own_hidden, w_value, preferred_element_type=jnp.float32).astype(jnp.bfloat16)
        angles = rope_angles(own_lengths, head_dim)
        q_heads = q_rows.reshape(rows_dev, num_heads, head_dim).astype(jnp.float32)
        q_rot = apply_rope(q_heads, angles[:, None, :]).astype(jnp.bfloat16)
        k_rot = apply_rope(k_new.astype(jnp.float32), angles).astype(jnp.bfloat16)
        new_slot = (lax.broadcasted_iota(jnp.int32, (1, seq_len), 1) == own_lengths[:, None])[:, :, None]
        k_out = jnp.where(new_slot, k_rot[:, None, :], k_cache)
        v_out = jnp.where(new_slot, v_new[:, None, :], v_cache)
        attn_out = attend(q_rot, k_out, v_out, own_lengths)
        o_cols = lax.all_to_all(attn_out.reshape(rows_dev, num_heads * head_dim), 'tp', 1, 0, tiled=True)
        y_part = jnp.dot(o_cols, w_out, preferred_element_type=jnp.float32).astype(jnp.bfloat16)
        y_local = lax.psum_scatter(y_part, 'tp', scatter_dimension=1, tiled=True)
        return y_local, k_out, v_out

    return jax.shard_map(
        local_step,
        mesh=mesh,
        in_specs=(P('dp', None), P(None, 'tp'), P(), P(), P('tp', None), cache_spec, cache_spec, P('dp')),
        out_specs=(P('dp', 'tp'), cache_spec, cache_spec),
        check_vma=False,
    )
```

profile of v0, /device:TPU:30, one launch (start us, length us, event | category | flops | bytes accessed | tf_op | source)
XLA Modules:
  0.0 131.5 jit_solution(17081993228267930915)
XLA Ops:
  7.2 0.0 copy-start.3
  7.2 7.7 %convolution_convert_fusion.1 = bf16[256,512]{1,0:T(8,128)(2,1)} fusion(bf16[256,8192]{1,0:T(8,128)(2,1)} %param.8, bf16[8192,512]{1,0:T(8,128)(2,1)} %param.9), kind=kOutput, calls=%fused_computation.7 | convolution fusion | flops 2147614720 | bytes 12845056 | tf_op jit(solution)/shard_map/dot_general | solution.py:44
  14.9 9.6 %all-to-all-start = ((bf16[16,16,512]{2,1,0:T(8,128)(2,1)}), bf16[16,16,512]{2,1,0:T(8,128)(2,1)S(1)}, u32[]{:S(2)}, u32[]{:S(2)}) async-start(bf16[16,16,512]{2,1,0:T(8,128)(2,1)} %bitcast), calls=%async_computation | async-start | bytes 524288 | tf_op jit(solution)/shard_map/all_to_all | solution.py:45
  24.5 0.1 reduce-scatter.2.cloned.1.call-start
  24.6 0.0 copy-done.3
  24.6 0.1 fusion.15
  24.7 0.0 copy-start.1
  24.7 0.0 copy-start.2
  24.7 3.1 %convolution_convert_fusion.2 = bf16[16,256]{1,0:T(8,128)(2,1)S(1)} fusion(bf16[8192,256]{1,0:T(8,128)(2,1)} %param.11, bf16[256,8192]{1,0:T(8,128)(2,1)} %param.8, s32[]{:T(128)S(6)} %select_n.15), kind=kOutput, calls=%fused_computation.8 | convolution fusion | flops 67112960 | bytes 4464644 | tf_op jit(solution)/shard_map/dot_general | solution.py:49
  27.7 3.6 %fusion.2 = f32[16,256]{1,0:T(8,128)S(1)} fusion(bf16[8192,256]{1,0:T(8,128)(2,1)} %param.10, bf16[256,8192]{1,0:T(8,128)(2,1)} %param.8, s32[]{:T(128)S(6)} %select_n.15), kind=kOutput, calls=%fused_computation.10 | convolution fusion | flops 67117056 | bytes 4472836 | tf_op jit(solution)/shard_map/dot_general | solution.py:48
  31.4 0.1 iota_compare_fusion.1
  31.5 0.1 multiply_cosine_fusion
  31.6 0.0 copy-done.1
  31.6 0.0 copy-done.2
  31.6 4.0 %broadcast_select_fusion.1 = (bf16[16,512,256]{2,1,0:T(8,128)(2,1)}, bf16[16,512,256]{2,1,0:T(8,128)(2,1)}) fusion(bf16[16,512,256]{2,1,0:T(8,128)(2,1)S(1)} %copy-done.1, pred[16,512]{1,0:T(8,128)(4,1)S(1)} %get-tuple-element.16, bf16[16,256]{1,0:T(8,128)(2,1)S(1)} %pad_maximum_fusion, bf16[16,512,256]{2,1,0:T(8,128)(2,1)S(1)} %copy-done.2, ...), kind=kLoop, calls=%fused_computation.2 | loop fusion | flops 4194304 | bytes 16801792 | tf_op jit(solution)/shard_map/jit(_where)/select_n | solution.py:55
  35.6 0.0 all-to-all-done
  35.6 0.1 convert_bitcast_fusion
  35.7 0.3 copy.12
  36.0 0.1 reshape.132
  36.1 0.0 copy-start
  36.1 0.1 subtract_convert_fusion
  36.2 3.8 %fusion.16 = (f32[16,32]{1,0:T(8,128)S(1)}, f32[16,32,512]{2,1,0:T(8,128)S(1)}) fusion(bf16[16,512,256]{2,1,0:T(8,128)(2,1)} %get-tuple-element.9, bf16[16,32,128]{2,1,0:T(8,128)(2,1)S(1)} %get-tuple-element.6, bf16[16,32,128]{2,1,0:T(8,128)(2,1)S(1)} %get-tuple-element.5, pred[16,512]{1,0:T(8,128)(4,1)S(1)} %get-tuple-element.15), kind=kOutput, calls=%fused_computation.35 | convolution fusion | flops 135527936 | bytes 5515264 | tf_op jit(solution)/shard_map/bhd,bsd->bhs/dot_general | solution.py:25
  40.0 0.4 fusion.3
  40.3 0.0 copy-done
  40.3 0.9 fusion.1
  41.2 0.1 all_to_all.26
  41.3 0.2 copy.13
  41.5 17.8 %all_to_all.32 = bf16[16,16,512]{2,0,1:T(8,128)(2,1)S(1)} all-to-all(bf16[16,16,512]{2,0,1:T(8,128)(2,1)S(1)} %copy.13), channel_id=1, replica_groups=mesh['dp'=4,'tp'=16] {'tp'}, dimensions={1} | all-to-all | bytes 524288 | tf_op jit(solution)/shard_map/all_to_all | solution.py:58
  59.3 7.7 %convolution_convert_fusion = bf16[256,8192]{1,0:T(8,128)(2,1)} fusion(bf16[256,512]{1,0:T(8,128)(2,1)S(1)} %bitcast.14, bf16[512,8192]{1,0:T(8,128)(2,1)} %param.12), kind=kOutput, calls=%fused_computation | convolution fusion | flops 2149580800 | bytes 12845056 | tf_op jit(solution)/shard_map/dot_general | solution.py:59
  66.9 0.1 reduce-scatter.2.cloned.1.call-update
  67.0 57.6 %reduce-scatter.2.cloned.1.call-done = bf16[256,512]{1,0:T(8,128)(2,1)} async-done(((bf16[256,8192]{1,0:T(8,128)(2,1)}), bf16[256,512]{1,0:T(8,128)(2,1)}) %reduce-scatter.2.cloned.1.call-update) | async-done | bytes 262160 | tf_op jit(solution)/shard_map/reduce_scatter | solution.py:60
  (2 shorter events, 0.0 us)
Async XLA Ops:
  7.2 17.4 %copy-start.3 = (s32[256]{0:T(256)S(1)}, s32[256]{0:T(256)}, u32[]{:S(2)}) copy-start(s32[256]{0:T(256)} %param.15) | copy-start | bytes 3076
  14.9 20.8 %all-to-all-start = ((bf16[16,16,512]{2,1,0:T(8,128)(2,1)}), bf16[16,16,512]{2,1,0:T(8,128)(2,1)S(1)}, u32[]{:S(2)}, u32[]{:S(2)}) async-start(bf16[16,16,512]{2,1,0:T(8,128)(2,1)} %bitcast), calls=%async_computation | async-start | bytes 524288 | tf_op jit(solution)/shard_map/all_to_all | solution.py:45
  24.5 100.2 %reduce-scatter.2.cloned.1.call-start = ((), (), s32[]{:S(2)}) async-start(), calls=%async_computation.3 | async-start | bytes 4456448 | tf_op jit(solution)/shard_map/reduce_scatter | solution.py:60
  24.7 6.9 %copy-start.1 = (bf16[16,512,256]{2,1,0:T(8,128)(2,1)S(1)}, bf16[16,512,256]{2,1,0:T(8,128)(2,1)}, u32[]{:S(2)}) copy-start(bf16[16,512,256]{2,1,0:T(8,128)(2,1)} %param.13) | copy-start | bytes 12582916
  24.7 6.9 %copy-start.2 = (bf16[16,512,256]{2,1,0:T(8,128)(2,1)S(1)}, bf16[16,512,256]{2,1,0:T(8,128)(2,1)}, u32[]{:S(2)}) copy-start(bf16[16,512,256]{2,1,0:T(8,128)(2,1)} %param.14) | copy-start | bytes 12582916
  36.1 4.2 %copy-start = (bf16[16,512,256]{2,1,0:T(8,128)(2,1)S(1)}, bf16[16,512,256]{2,1,0:T(8,128)(2,1)}, u32[]{:S(2)}) copy-start(bf16[16,512,256]{2,1,0:T(8,128)(2,1)} %get-tuple-element.10) | copy-start | bytes 12582916
Sparse Core Ops, SparseCore 0:
  67.1 57.4 reduce-scatter.1
where the time goes:
time: 132 us
  waiting for transfers between devices  57.7 us (44%)
  matrix products  26.8 us (20%)
  blocking collectives  17.8 us (13%)
  between operations  14.2 us (11%)
  starting transfers between devices  9.66 us (7%)
  other arithmetic  4.79 us (4%)
    reduce_scatter x1, waiting for transfers between devices, local_step(): y_local = lax.psum_scatter(y_part, 'tp', scatter_dimension=1, tiled=True)  57.6 us
    all_to_all x1, blocking collectives, local_step(): lax.all_to_all(attn_out.reshape(rows_dev, num_heads * head_dim), 'tp', 1,...  17.8 us
    all_to_all x1, starting transfers between devices, local_step(): q_rows = lax.all_to_all(q_cols, 'tp', 0, 1, tiled=True)  9.6 us
    dot_general x1, matrix products, local_step(): jnp.dot(hidden, w_query, preferred_element_type=jnp.float32)  7.69 us
    dot_general x1, matrix products, local_step(): jnp.dot(o_cols, w_out, preferred_element_type=jnp.float32)  7.68 us
    select_n x1, other arithmetic, local_step(): k_out = jnp.where(new_slot, k_rot[:, None, :], k_cache)  4 us
    dot_general x1, matrix products, attend(): jnp.einsum('bhd,bsd->bhs', q_rot, k_all, preferred_element_type=jnp.float32)  3.77 us
    dot_general x1, matrix products, local_step(): jnp.dot(own_hidden, w_key, preferred_element_type=jnp.float32)  3.64 us
  transfers between devices with their start and end apart: 2, of which 1 were waited for; matrix products, arithmetic and copies ran while one was open for 8% of the time, Pallas kernels for 0%

commit v1 on v0

v1 whole, which is shorter than its diff:
```python
import functools

import jax
import jax.numpy as jnp
from jax import lax
from jax.experimental import pallas as pl
from jax.experimental.pallas import tpu as pltpu
from jax.sharding import PartitionSpec as P

MESH = pl.DeviceIdType.MESH
HALVES = 2
K_CHUNKS = 8
F32 = jnp.float32
BF16 = jnp.bfloat16


def rope_angles(positions, head_dim):
    half_dim = head_dim // 2
    inv_freq = 10000.0 ** (-(jnp.arange(half_dim, dtype=jnp.float32) * 2.0) / head_dim)
    return positions.astype(jnp.float32)[:, None] * inv_freq[None, :]


def decode_kernel(
    n, hid_hbm, wq_hbm, wk_hbm, wv_hbm, wo_hbm, kc_hbm, vc_hbm, cos_ref, sin_ref, len_ref,
    y_ref, knew_ref, vnew_ref,
    hid, wq, wk, wv, wo, kc, vc, acc, qs, qr, q_lo, q_hi, o_lo, o_hi, osend, orecv, kf, vf,
    pm, ps, pr, rs, rr,
    sem_h, sem_w, sem_kv, sem_kc, sem_vc, sem_wo, q_ssem, q_rsem, o_ssem, o_rsem, p_ssem, p_rsem, r_ssem, r_rsem,
):
    me = lax.axis_index("tp")
    chips = n // 2
    core = lax.rem(me, 2)
    chip = me // 2
    partner = me + 1 - 2 * core
    right = lax.rem(me + 2, n)
    left = lax.rem(me + n - 2, n)
    neighbours = (right, left)

    batch, depth = hid.shape
    cols = wq.shape[1]
    rows = batch // n
    half_rows = rows // HALVES
    seq_len, head_dim = kc.shape[1:]
    half_dim = head_dim // 2
    dev_heads = cols // head_dim
    heads = dev_heads * n
    block = depth // K_CHUNKS
    part = cols // 2
    scale = head_dim ** -0.5

    barrier = pltpu.get_barrier_semaphore()

    def greet(i, carry):
        pl.semaphore_signal(barrier, inc=1, device_id={"tp": lax.rem(me + i, n)}, device_id_type=MESH)
        return carry

    lax.fori_loop(1, n, greet, 0)

    def load_h(i):
        return pltpu.make_async_copy(hid_hbm.at[:, pl.ds(i * block, block)], hid.at[:, pl.ds(i * block, block)], sem_h.at[i])

    def load_w(i):
        return pltpu.make_async_copy(wq_hbm.at[pl.ds(i * block, block)], wq.at[pl.ds(i * block, block)], sem_w.at[i])

    def load_cache(hbm, vmem, sem, h):
        return pltpu.make_async_copy(hbm.at[pl.ds(h * half_rows, half_rows)], vmem.at[pl.ds(h * half_rows, half_rows)], sem.at[h])

    wk_copy = pltpu.make_async_copy(wk_hbm, wk, sem_kv.at[0])
    wv_copy = pltpu.make_async_copy(wv_hbm, wv, sem_kv.at[1])
    wo_copy = pltpu.make_async_copy(wo_hbm, wo, sem_wo.at[0])

    for i in range(K_CHUNKS):
        load_h(i).start()
        load_w(i).start()
    acc[...] = jnp.zeros_like(acc)

    def q_step(i):
        span = pl.ds(pl.multiple_of(i * block, block), block)
        acc[...] += jnp.dot(hid[:, span], wq[span, :], preferred_element_type=F32)

    for i in range(K_CHUNKS):
        load_h(i).wait()
        load_w(i).wait()
        if i == K_CHUNKS - 2:
            wk_copy.start()
            wv_copy.start()
            for h in range(HALVES):
                load_cache(kc_hbm, kc, sem_kc, h).start()
                load_cache(vc_hbm, vc, sem_vc, h).start()
            wo_copy.start()
        q_step(i)

    q_all = acc[...].reshape(n, HALVES, half_rows, cols)
    for h in range(HALVES):
        qs[h] = q_all[:, h].astype(BF16)

    pl.semaphore_wait(barrier, n - 1)

    def exchange(src, dst, send_sem, recv_sem, h):
        def send(i, carry):
            peer = lax.rem(me + i, n)
            pltpu.make_async_remote_copy(
                src_ref=src.at[h, peer],
                dst_ref=dst.at[h, me],
                send_sem=send_sem.at[h],
                recv_sem=recv_sem.at[h],
                device_id={"tp": peer},
                device_id_type=MESH,
            ).start()
            return carry

        lax.fori_loop(1, n, send, 0)
        dst[h, me] = src[h, me]

    def exchange_wait(buf, sem, h):
        others = buf.at[h, pl.ds(0, n - 1)]
        pltpu.make_async_copy(others, others, sem.at[h]).wait()

    for h in range(HALVES):
        exchange(qs, qr, q_ssem, q_rsem, h)

    wk_copy.wait()
    wv_copy.wait()
    own = pl.ds(pl.multiple_of(me * rows, rows), rows)

    def kv_step(i, carry):
        k_sum, v_sum = carry
        span = pl.ds(pl.multiple_of(i * block, block), block)
        h_own = hid[own, span]
        return (
            k_sum + jnp.dot(h_own, wk[span, :], preferred_element_type=F32),
            v_sum + jnp.dot(h_own, wv[span, :], preferred_element_type=F32),
        )

    zero = jnp.zeros((rows, head_dim), F32)
    k_sum, v_sum = lax.fori_loop(0, K_CHUNKS, kv_step, (zero, zero))
    k_full = k_sum.astype(BF16).astype(F32)
    cosines, sines = cos_ref[...], sin_ref[...]
    k_lo, k_hi = k_full[:, :half_dim], k_full[:, half_dim:]
    k_rot = jnp.concatenate([k_lo * cosines - k_hi * sines, k_hi * cosines + k_lo * sines], axis=-1).astype(BF16)
    knew_ref[...] = k_rot
    vnew_ref[...] = v_sum.astype(BF16)
    kf[...] = k_rot.astype(F32)
    vf[...] = v_sum.astype(BF16).astype(F32)

    slots = lax.broadcasted_iota(jnp.int32, (heads, seq_len), 1)

    def attend(h):
        exchange_wait(qr, q_rsem, h)
        span = pl.ds(h * half_rows, half_rows)
        cosines, sines = cos_ref[span, :], sin_ref[span, :]
        for src in range(n):
            for j in range(dev_heads):
                x = qr[h, src, :, pl.ds(j * head_dim, head_dim)].astype(F32)
                lo, hi = x[:, :half_dim], x[:, half_dim:]
                place = pl.ds(src * dev_heads + j, half_rows, stride=heads)
                q_lo[place, :] = lo * cosines - hi * sines
                q_hi[place, :] = hi * cosines + lo * sines
        load_cache(kc_hbm, kc, sem_kc, h).wait()
        load_cache(vc_hbm, vc, sem_vc, h).wait()
        for r in range(half_rows):
            b = h * half_rows + r
            at = pl.ds(r * heads, heads)
            q = jnp.concatenate([q_lo[at, :], q_hi[at, :]], axis=-1).astype(BF16)
            length = len_ref[me * rows + b]
            k_row, v_row = kf[pl.ds(b, 1), :], vf[pl.ds(b, 1), :]
            s = lax.dot_general(q, kc[b], (((1,), (1,)), ((), ())), preferred_element_type=F32) * scale
            s_new = jnp.sum(q.astype(F32) * k_row, axis=-1, keepdims=True) * scale
            s = jnp.where(slots < length, s, -1e30)
            top = jnp.maximum(jnp.max(s, axis=-1, keepdims=True), s_new)
            e = jnp.where(slots < length, jnp.exp(s - top), 0.0)
            e_new = jnp.exp(s_new - top)
            total = jnp.sum(e, axis=-1, keepdims=True) + e_new
            o = jnp.dot(e.astype(BF16), vc[b], preferred_element_type=F32)
            o = (o + e_new.astype(BF16).astype(F32) * v_row) / total
            o_lo[at, :] = o[:, :half_dim]
            o_hi[at, :] = o[:, half_dim:]
        for dst in range(n):
            for j in range(dev_heads):
                place = pl.ds(dst * dev_heads + j, half_rows, stride=heads)
                osend[h, dst, :, pl.ds(j * head_dim, half_dim)] = o_lo[place, :].astype(BF16)
                osend[h, dst, :, pl.ds(j * head_dim + half_dim, half_dim)] = o_hi[place, :].astype(BF16)
        exchange(osend, orecv, o_ssem, o_rsem, h)

    for h in range(HALVES):
        attend(h)

    wo_copy.wait()

    def owner(k, way):
        return lax.rem(chip + chips - 1 - k, chips) if way == 0 else lax.rem(chip + 1 + k, chips)

    def partner_copy(h, k):
        return pltpu.make_async_remote_copy(
            src_ref=ps.at[h, k], dst_ref=pr.at[h, k], send_sem=p_ssem.at[h], recv_sem=p_rsem.at[h, k],
            device_id={"tp": partner}, device_id_type=MESH,
        )

    def multiply(h, k):
        o_cols = orecv[h].reshape(n * half_rows, cols)
        for way in range(2):
            base = owner(k, way) * 2
            other = pl.ds(pl.multiple_of((base + 1 - core) * cols + way * part, part), part)
            mine = pl.ds(pl.multiple_of((base + core) * cols + way * part, part), part)
            ps[h, k, way] = jnp.dot(o_cols, wo[:, other], preferred_element_type=F32).astype(BF16)
            pm[h, k, way] = jnp.dot(o_cols, wo[:, mine], preferred_element_type=F32)
        partner_copy(h, k).start()

    def ring_copy(h, k, way):
        return pltpu.make_async_remote_copy(
            src_ref=rs.at[h, k, way], dst_ref=rr.at[h, k, way], send_sem=r_ssem.at[h], recv_sem=r_rsem.at[h, k, way],
            device_id={"tp": neighbours[way]}, device_id_type=MESH,
        )

    def reduce_step(h, k):
        partner_copy(h, k).wait_recv()
        for way in range(2):
            value = pm[h, k, way] + pr[h, k, way].astype(F32)
            if k > 0:
                ring_copy(h, k - 1, way).wait_recv()
                value = value + rr[h, k - 1, way].astype(F32)
            if k < chips - 1:
                rs[h, k, way] = value.astype(BF16)
                ring_copy(h, k, way).start()
            else:
                out = value.astype(BF16) if HALVES == 1 else value
                y_ref[:, h, :, pl.ds(way * part, part)] = out.reshape(n, half_rows, part).astype(BF16)

    def multiplies(h, lo, hi):
        def body(k, carry):
            multiply(h, k)
            return carry

        lax.fori_loop(lo, hi, body, 0)

    for h in range(HALVES):
        exchange_wait(orecv, o_rsem, h)
        multiplies(h, 0, 2)
        reduce_step(h, 0)
        if h == 0:
            multiplies(h, 2, chips)
    reduce_step(0, 1)
    for h in range(1, HALVES):
        multiplies(h, 2, chips)
    for k in range(1, chips):
        for h in range(HALVES):
            if (h, k) != (0, 1):
                reduce_step(h, k)

    for h in range(HALVES):
        exchange_wait(qs, q_ssem, h)
        exchange_wait(osend, o_ssem, h)
        pltpu.make_async_copy(ps.at[h], ps.at[h], p_ssem.at[h]).wait()
        pltpu.make_async_copy(rs.at[h], rs.at[h], r_ssem.at[h]).wait()


def solution(mesh):
    n = mesh.shape["tp"]
    cache_spec = P(("dp", "tp"), None, None)

    def local_step(hidden, w_query, w_key, w_value, w_out, k_cache, v_cache, lengths):
        rows, seq_len, head_dim = k_cache.shape
        batch, depth = hidden.shape
        cols = w_query.shape[1]
        half_rows = rows // HALVES
        chips = n // 2
        part = cols // 2
        heads = cols * n // head_dim
        half_dim = head_dim // 2
        own_lengths = lax.dynamic_slice_in_dim(lengths, lax.axis_index("tp") * rows, rows, axis=0)
        angles = rope_angles(own_lengths, head_dim)
        any_spec = pl.BlockSpec(memory_space=pl.ANY)
        vmem_spec = pl.BlockSpec(memory_space=pltpu.VMEM)
        smem_spec = pl.BlockSpec(memory_space=pltpu.SMEM)
        dma = pltpu.SemaphoreType.DMA
        piece = (n * half_rows, part)
        y, k_new, v_new = pl.pallas_call(
            functools.partial(decode_kernel, n),
            out_shape=(
                jax.ShapeDtypeStruct((n, HALVES, half_rows, cols), BF16),
                jax.ShapeDtypeStruct((rows, head_dim), BF16),
                jax.ShapeDtypeStruct((rows, head_dim), BF16),
            ),
            in_specs=[any_spec] * 7 + [vmem_spec, vmem_spec, smem_spec],
            out_specs=(vmem_spec, vmem_spec, vmem_spec),
            scratch_shapes=[
                pltpu.VMEM((batch, depth), BF16),
                pltpu.VMEM((depth, cols), BF16),
                pltpu.VMEM((depth, head_dim), BF16),
                pltpu.VMEM((depth, head_dim), BF16),
                pltpu.VMEM(w_out.shape, BF16),
                pltpu.VMEM(k_cache.shape, BF16),
                pltpu.VMEM(v_cache.shape, BF16),
                pltpu.VMEM((batch, cols), F32),
                pltpu.VMEM((HALVES, n, half_rows, cols), BF16),
                pltpu.VMEM((HALVES, n, half_rows, cols), BF16),
                pltpu.VMEM((half_rows * heads, half_dim), F32),
                pltpu.VMEM((half_rows * heads, half_dim), F32),
                pltpu.VMEM((half_rows * heads, half_dim), F32),
                pltpu.VMEM((half_rows * heads, half_dim), F32),
                pltpu.VMEM((HALVES, n, half_rows, cols), BF16),
                pltpu.VMEM((HALVES, n, half_rows, cols), BF16),
                pltpu.VMEM((rows, head_dim), F32),
                pltpu.VMEM((rows, head_dim), F32),
                pltpu.VMEM((HALVES, chips, 2) + piece, F32),
                pltpu.VMEM((HALVES, chips, 2) + piece, BF16),
                pltpu.VMEM((HALVES, chips, 2) + piece, BF16),
                pltpu.VMEM((HALVES, chips - 1, 2) + piece, BF16),
                pltpu.VMEM((HALVES, chips - 1, 2) + piece, BF16),
                dma((K_CHUNKS,)),
                dma((K_CHUNKS,)),
                dma((2,)),
                dma((HALVES,)),
                dma((HALVES,)),
                dma((1,)),
                dma((HALVES,)),
                dma((HALVES,)),
                dma((HALVES,)),
                dma((HALVES,)),
                dma((HALVES,)),
                dma((HALVES, chips)),
                dma((HALVES,)),
                dma((HALVES, chips - 1, 2)),
            ],
            compiler_params=pltpu.CompilerParams(
                collective_id=0, has_side_effects=True, vmem_limit_bytes=52 * 1024 * 1024
            ),
        )(hidden, w_query, w_key, w_value, w_out, k_cache, v_cache, jnp.cos(angles), jnp.sin(angles), lengths)
        new_slot = (lax.broadcasted_iota(jnp.int32, (1, seq_len), 1) == own_lengths[:, None])[:, :, None]
        k_out = jnp.where(new_slot, k_new[:, None, :], k_cache)
        v_out = jnp.where(new_slot, v_new[:, None, :], v_cache)
        return y.reshape(batch, cols), k_out, v_out

    return jax.shard_map(
        local_step,
        mesh=mesh,
        in_specs=(P("dp", None), P(None, "tp"), P(), P(), P("tp", None), cache_spec, cache_spec, P("dp")),
        out_specs=(P("dp", "tp"), cache_spec, cache_spec),
        check_vma=False,
    )
```

time: 132 us -> 67.6 us (0.51)
  Pallas kernels: 0 us -> 60.4 us
  waiting for transfers between devices: 57.7 us -> 0 us
  matrix products: 26.8 us -> 0 us
  blocking collectives: 17.8 us -> 0 us
  between operations: 14.2 us -> 0.68 us
  starting transfers between devices: 9.66 us -> 0 us
    pallas_call x0 -> x1, Pallas kernels: none -> 60.4 us  [local_step(): pl.pallas_call(functools.partial(decode_kernel, n), out_shape=(jax.ShapeD...]
    reduce_scatter x1 -> x0, waiting for transfers between devices: 57.6 us -> none  [local_step(): y_local = lax.psum_scatter(y_part, 'tp', scatter_dimension=1, tiled=True)]
    dot_general x6 -> x0, matrix products: 26.8 us -> none  [the longest x1 7.69 us: local_step(): jnp.dot(hidden, w_query, preferred_element_type=jnp.float32)]
    all_to_all x1 -> x0, blocking collectives: 17.8 us -> none  [local_step(): lax.all_to_all(attn_out.reshape(rows_dev, num_heads * head_dim), 'tp', 1,...]
    all_to_all x1 -> x0, starting transfers between devices: 9.6 us -> none  [local_step(): q_rows = lax.all_to_all(q_cols, 'tp', 0, 1, tiled=True)]
    unnamed x8 -> x7, local copies, waits for them, and re-layouts: 0.02 us -> 1.38 us
  transfers between devices with their start and end apart: 2 -> 0, of which waited for: 1 -> 0; matrix products, arithmetic and copies ran while one was open for 8% -> 0% of each run, Pallas kernels for 0% -> 0%
where the time goes in v1:
time: 67.6 us; the launch traced here: 67.5 us
  Pallas kernels  60.4 us (89%)
  other arithmetic  4.97 us (7%)
  local copies, waits for them, and re-layouts  1.38 us (2%)
  between operations  0.68 us (1%)
    pallas_call x1, Pallas kernels, local_step(): pl.pallas_call(functools.partial(decode_kernel, n), out_shape=(jax.ShapeD...  60.4 us
    select_n x1, other arithmetic, local_step(): v_out = jnp.where(new_slot, v_new[:, None, :], v_cache)  4 us
    unnamed x7, local copies, waits for them, and re-layouts  1.38 us

profile of v1, /device:TPU:30, one launch (start us, length us, event | category | flops | bytes accessed | tf_op | source)
XLA Modules:
  0.0 67.5 jit_solution(13921369284038002710)
XLA Ops:
  0.6 0.8 %fusion = (f32[16]{0:T(128)S(1)}, s32[16]{0:T(128)S(1)}) fusion(s32[256]{0:T(256)} %len_ref.1, s32[]{:T(128)S(6)} %select_n.10), kind=kLoop, calls=%fused_computation.6 | loop fusion | flops 16 | bytes 196 | tf_op jit(solution)/shard_map/convert_element_type | solution.py:20
  1.4 0.1 iota_compare_fusion
  1.5 0.1 multiply_sine_fusion
  1.6 0.0 copy-start
  1.6 0.7 copy-done
  2.3 0.0 copy-start.1
  2.3 0.0 copy-start.2
  2.3 60.4 %shard_map.103 = (bf16[16,2,8,512]{3,2,1,0:T(8,128)(2,1)S(1)}, bf16[16,256]{1,0:T(8,128)(2,1)S(1)}, bf16[16,256]{1,0:T(8,128)(2,1)S(1)}) custom-call(bf16[256,8192]{1,0:T(8,128)(2,1)} %hid_hbm.1, bf16[8192,512]{1,0:T(8,128)(2,1)} %wq_hbm.1, bf16[8192,256]{1,0:T(8,128)(2,1)} %wk_hbm.1, bf16[8192,256]{1,0:T(8,128)(2,1)} %wv_hbm.1, bf16[512,8192]{1,0:T(8,128)(2,1)} %wo_hbm.1, ...), custom_call_target="tpu_custom_call" | custom-call | tf_op jit(solution)/shard_map/pallas_call | solution.py:277
  62.7 0.0 copy-done.1
  62.7 0.0 copy-done.2
  62.8 4.0 %broadcast_select_fusion = (bf16[16,512,256]{2,1,0:T(8,128)(2,1)}, bf16[16,512,256]{2,1,0:T(8,128)(2,1)}) fusion(bf16[16,512,256]{2,1,0:T(8,128)(2,1)S(1)} %copy-done.2, pred[16,512]{1,0:T(8,128)(4,1)S(1)} %iota_compare_fusion, bf16[16,256]{1,0:T(8,128)(2,1)S(1)} %get-tuple-element.8, bf16[16,512,256]{2,1,0:T(8,128)(2,1)S(1)} %copy-done.1, ...), kind=kLoop, calls=%fused_computation | loop fusion | flops 4194304 | bytes 16801792 | tf_op jit(solution)/shard_map/jit(_where)/select_n | solution.py:331
  66.8 0.7 %copy.12 = bf16[256,512]{1,0:T(8,128)(2,1)} copy(bf16[256,512]{1,0:T(8,128)(2,1)S(1)} %bitcast.1) | data formatting | bytes 524288
  (1 shorter events, 0.0 us)
Async XLA Ops:
  1.6 0.7 %copy-start = (s32[256]{0:T(256)S(1)}, s32[256]{0:T(256)}, u32[]{:S(2)}) copy-start(s32[256]{0:T(256)} %len_ref.1) | copy-start | bytes 3076
  2.3 60.4 %copy-start.1 = (bf16[16,512,256]{2,1,0:T(8,128)(2,1)S(1)}, bf16[16,512,256]{2,1,0:T(8,128)(2,1)}, u32[]{:S(2)}) copy-start(bf16[16,512,256]{2,1,0:T(8,128)(2,1)} %kc_hbm.1) | copy-start | bytes 12582916
  2.3 60.5 %copy-start.2 = (bf16[16,512,256]{2,1,0:T(8,128)(2,1)S(1)}, bf16[16,512,256]{2,1,0:T(8,128)(2,1)}, u32[]{:S(2)}) copy-start(bf16[16,512,256]{2,1,0:T(8,128)(2,1)} %vc_hbm.1) | copy-start | bytes 12582916
